TPU v7x, 32 devices: a whole 2x2x4 slice. The times are simulated.
32 devices in a mesh: slab: 16 (over z, y, x), cell: 2 (over core).
Axes of the slice: x: 2, y: 2, z: 4, core: 2. Of those that a mesh axis runs over, the one named last changes fastest.
Arguments:
- cell_row: int32 [16384], P(('slab', 'cell')), may hold values from 0 to 2043, as said below
- cell_col: int32 [16384], P(('slab', 'cell')), may hold values from 0 to 2039
- cell_width: int32 [16384], P(('slab', 'cell')), may hold values from 1 to 8
- cell_height: int32 [16384], P(('slab', 'cell')), may hold values from 1 to 4
- cell_region: int32 [16384], P(('slab', 'cell')), may hold values from 0 to 3
- cell_offset: float32 [2, 16384], P(None, ('slab', 'cell')), may hold values from 0 to 1
Outputs:
- field_x: float32 [4, 2048, 2048], P(None, ('slab', 'cell'))
- field_y: float32 [4, 2048, 2048], P(None, ('slab', 'cell'))
- cell_force: float32 [2, 16384], P(None, ('slab', 'cell'))
- energy: float32 [], replicated
- overflow: float32 [], replicated
Inputs may be any that keep to these rules, and one draw needn't show every extreme that they name: `cell_row`: cell i belongs to row slab s = i // 1024: its row lies in [s * 128, (s + 1) * 128); cells of the last slab lie at least 4 rows below the top of the grid.
All inputs are finite; a program needn't handle non-finite values.
Results may differ from a plain program's by a relative error of at most 0.0015.
Values may be sent and summed in bfloat16 or wider, within the bound.
A program may use at most 128 MiB of HBM per device.

v0:
```python
import functools
import math

import jax
import jax.numpy as jnp
import numpy as np
from jax import lax
from jax.experimental import pallas as pl
from jax.experimental.pallas import tpu as pltpu
from jax.sharding import PartitionSpec as P

M = 2048
REGIONS = 4
SEND_SCALE = 0.125


def shifted(value, axis, steps):
    count = lax.axis_size(axis)
    first, last = (max(0, -steps), min(count, count - steps))
    return lax.ppermute(value, axis, [(source, source + steps) for source in range(first, last)])


def intersect(offset_bins, fraction, extent):
    high_edge = jnp.minimum(offset_bins + 1.0, fraction + extent)
    low_edge = jnp.maximum(offset_bins, fraction)
    return jnp.maximum(high_edge - low_edge, 0.0).astype(jnp.bfloat16)


def basis_tables(length):
    inner = 32
    outer = length // 2 // inner
    position = 2 * lax.iota(jnp.int32, length) + 1

    def small(freq):
        phase = freq[..., None] * position % (4 * length)
        angle = phase.astype(jnp.float32) * (math.pi / (2.0 * length))
        return jnp.cos(angle), jnp.sin(angle)

    coarse_cos, coarse_sin = small(2 * inner * lax.iota(jnp.int32, outer))
    parity = lax.iota(jnp.int32, 2)[:, None]
    fine_cos, fine_sin = small(2 * lax.iota(jnp.int32, inner)[None, :] + parity)
    coarse_cos, coarse_sin, fine_cos, fine_sin = lax.optimization_barrier(
        (coarse_cos, coarse_sin, fine_cos, fine_sin)
    )
    def build(left_a, right_a, left_b, right_b, sign):
        step_rows = min(4, outer) * inner

        def kernel(la, ra, lb, rb, out):
            step = pl.program_id(1)
            for part in range(step_rows // inner):
                at = pl.ds(step * (step_rows // inner) + part, 1)
                value = la[at, :] * ra[0] + sign * (lb[at, :] * rb[0])
                value = value * math.sqrt(2.0 / length)
                if part == 0:
                    first = (pl.program_id(0) == 0) & (step == 0)
                    here = lax.broadcasted_iota(jnp.int32, (inner, length), 0) == 0
                    value = jnp.where(first & here, value * math.sqrt(0.5), value)
                out[pl.ds(part * inner, inner), :] = value

        small_spec = pl.BlockSpec((outer, length), lambda p, i: (0, 0))
        fine_spec = pl.BlockSpec((1, inner, length), lambda p, i: (p, 0, 0))
        steps = outer * inner // step_rows
        return pl.pallas_call(
            kernel,
            out_shape=jax.ShapeDtypeStruct((length, length), jnp.float32),
            grid=(2, steps),
            in_specs=[small_spec, fine_spec, small_spec, fine_spec],
            out_specs=pl.BlockSpec((step_rows, length), lambda p, i: (p * steps + i, 0)),
            cost_estimate=pl.CostEstimate(
                flops=4 * length * length, bytes_accessed=4 * length * length, transcendentals=0
            ),
        )(left_a, right_a, left_b, right_b)

    cosine = build(coarse_cos, fine_cos, coarse_sin, fine_sin, -1.0)
    sine = build(coarse_sin, fine_cos, coarse_cos, fine_sin, 1.0)
    return cosine, sine


def frequency_order(index, length):
    half = length // 2
    return jnp.where(index < half, 2 * index, 2 * (index - half) + 1)


def matmul(left, right, contract):
    return lax.dot_general(
        left,
        right,
        (contract, ((), ())),
        precision=lax.Precision.HIGH,
        preferred_element_type=jnp.float32,
    )


def body(cell_row, cell_col, cell_width, cell_height, cell_region, cell_offset):
    slab_count = lax.axis_size("slab")
    cell_count = lax.axis_size("cell")
    slab_index = lax.axis_index("slab")
    cell_index = lax.axis_index("cell")
    device_count = slab_count * cell_count
    length = M
    regions = REGIONS
    own_regions = regions // cell_count
    rows = length // device_count
    width = length // slab_count
    cells = cell_row.shape[0]
    base_row = (slab_index * cell_count + cell_index) * rows
    everyone = ("slab", "cell")
    cosine, sine = basis_tables(length)

    table = jnp.concatenate(
        [jnp.stack([cell_row, cell_col, cell_width, cell_height, cell_region]).astype(jnp.float32), cell_offset]
    )
    slab_cells = lax.all_gather(table, "cell", axis=1, tiled=True)
    below = shifted(slab_cells, "slab", 1)
    seen = jnp.concatenate([slab_cells, below], axis=1)
    row, col, wide, high, region, off_x, off_y = [seen[i][:, None] for i in range(7)]
    natural = lax.iota(jnp.float32, length)[None, :]
    x_intersect = intersect(natural - col, off_x, wide)
    y_bins = base_row.astype(jnp.float32) + lax.iota(jnp.float32, rows)[None, :] - row
    y_intersect = intersect(y_bins, off_y, high)
    region_hot = region == lax.iota(jnp.float32, regions)[None, :]
    y_region = jnp.where(region_hot[:, :, None], y_intersect[:, None, :], jnp.bfloat16(0)).reshape(
        seen.shape[1], regions * rows
    )
    density = lax.dot_general(
        y_region, x_intersect, (((0,), (0,)), ((), ())), preferred_element_type=jnp.float32
    )
    excess_local = jnp.sum(jnp.maximum(density - 1.0, 0.0))
    area_local = jnp.sum(density)

    by_freq_x = matmul(density, cosine, ((1,), (1,)))
    outgoing = by_freq_x.reshape(cell_count, own_regions, rows, slab_count, width)
    outgoing = outgoing.astype(jnp.float16)
    outgoing = outgoing.transpose(3, 0, 2, 1, 4).reshape(device_count, rows, own_regions * width)
    crossed = lax.all_to_all(outgoing, everyone, split_axis=0, concat_axis=0, tiled=True)
    crossed, sine = lax.optimization_barrier((crossed, sine))
    crossed = crossed.reshape(length, own_regions * width).astype(jnp.float32)
    spectrum = matmul(crossed, cosine, ((0,), (1,)))

    ky_int = frequency_order(lax.iota(jnp.int32, length), length)[None, :]
    kx_int = frequency_order(slab_index * width + lax.iota(jnp.int32, width), length)
    kx_int = jnp.tile(kx_int, own_regions)[:, None]
    kx, ky = kx_int.astype(jnp.float32), ky_int.astype(jnp.float32)
    at_anchor = kx_int + ky_int == 0
    step_size = math.pi / length
    squared = kx * kx + ky * ky
    potential_hat = jnp.where(
        at_anchor, 0.0, spectrum / (step_size * step_size * jnp.where(at_anchor, 1.0, squared))
    )
    energy_local = jnp.sum(spectrum * potential_hat) / (length * length)
    along_x = matmul(potential_hat * (step_size * kx * SEND_SCALE), cosine, ((1,), (0,)))
    along_y = matmul(potential_hat * (step_size * ky * SEND_SCALE), sine, ((1,), (0,)))

    def back(along):
        blocks = along.astype(jnp.float16).T.reshape(device_count, rows, own_regions * width)
        home = lax.all_to_all(blocks, everyone, split_axis=0, concat_axis=0, tiled=True)
        home = home.reshape(slab_count, cell_count, rows, own_regions, width)
        home = home.transpose(1, 3, 2, 0, 4).reshape(regions * rows, length)
        return home.astype(jnp.float32) * (1.0 / SEND_SCALE)

    home_x = back(along_x)
    home_y = back(along_y)
    sums = jnp.stack([excess_local, area_local, energy_local])
    sums, home_y = lax.optimization_barrier((sums, home_y))
    sums = jnp.broadcast_to(sums, (device_count, 3))
    sums = lax.all_to_all(sums, everyone, split_axis=0, concat_axis=0, tiled=True)
    field_x = matmul(home_x, sine, ((1,), (0,)))
    field_y = matmul(home_y, cosine, ((1,), (0,)))

    def pushed(field):
        sampled = lax.dot_general(
            x_intersect,
            field.astype(jnp.bfloat16),
            (((1,), (1,)), ((), ())),
            preferred_element_type=jnp.float32,
        )
        return jnp.sum(sampled * y_region.astype(jnp.float32), axis=1)

    partial = jnp.stack([pushed(field_x), pushed(field_y)])
    here, beneath = partial[:, : cells * cell_count], partial[:, cells * cell_count :]
    here = here + shifted(beneath, "slab", -1)
    here = here.reshape(2, cell_count, cells).transpose(1, 0, 2)
    cell_force = jnp.sum(lax.all_to_all(here, "cell", split_axis=0, concat_axis=0), axis=0)
    excess, area, energy = jnp.sum(sums, axis=0)
    shape = (regions, rows, length)
    return (field_x.reshape(shape), field_y.reshape(shape), cell_force, energy, excess / area)


INNER = 32
FINE = 48
LANES = 128
CODE_TOP = 32000.0


def trig(phase, length):
    angle = (phase % (4 * length)) * (math.pi / (2.0 * length))
    return np.cos(angle).astype(np.float32), np.sin(angle).astype(np.float32)


def small_tables(length):
    half = length // 2
    order = np.concatenate([2 * np.arange(half), 2 * np.arange(half) + 1])[None, :]
    coarse = np.arange(length // INNER)[:, None] * (2 * INNER)
    fine = 2 * np.arange(FINE)[:, None] + 1
    position = 2 * np.arange(half)[None, :] + 1
    freq_coarse = np.arange(half // INNER)[:, None] * (2 * INNER)
    freq_fine = (np.arange(2)[:, None, None] + 2 * np.arange(INNER)[None, :, None]) * position[None]
    return (
        trig(coarse * order, length)
        + trig(fine * order, length)
        + trig(freq_coarse * position, length)
        + trig(freq_fine, length)
    )


def split(value):
    high = value.astype(jnp.bfloat16)
    return high, (value - high.astype(jnp.float32)).astype(jnp.bfloat16)


def dot(left, right, contract=((1,), (0,))):
    return lax.dot_general(left, right, (contract, ((), ())), preferred_element_type=jnp.float32)


def overlap(steps, fraction, extent):
    high_edge = jnp.minimum(steps + 1.0, fraction + extent)
    return jnp.maximum(high_edge - jnp.maximum(steps, fraction), 0.0)


def row_iota(rows, columns):
    return lax.broadcasted_iota(jnp.int32, (rows, columns), 0).astype(jnp.float32)


def fold_rows(value):
    return jnp.sum(value.reshape(value.shape[0] // 8, 8, value.shape[1]), axis=0)


def fused_kernel(
    slab_count, length, cells, regions,
    table, ccos, csin, fcos, fsin, gcos, gsin, hcos, hsin,
    field_x, field_y, force, scalars,
    cells_all, xch, xcl, ych, ycl, ysh, ysl, draw, foh, fol, hxh, hxl, hyh, hyl,
    send_buf, send_scale, recv_buf, recv_scale, rounded, xf, xg, carry, yown, ybelow,
    energy_acc, excess_acc, area_acc, scal_out, scal_in, part_own, part_below, part_sib, part_up,
    cell_send, cell_recv, data_send, data_recv, scale_send, scale_recv,
    scal_send, scal_recv, part_send, part_recv,
):
    half = length // 2
    halves = slab_count // 2
    group = slab_count
    slab_rows = length // slab_count
    rows = slab_rows // 2
    both = 2 * cells
    device_count = 2 * slab_count
    slab = lax.axis_index("slab")
    core = lax.axis_index("cell")
    me = slab * 2 + core
    side = slab // halves
    spot = (slab % halves) * 2 + core
    f32, bf16 = jnp.float32, jnp.bfloat16

    def to(index):
        return (index // 2, index % 2)

    def cell_copy(step):
        return pltpu.make_async_remote_copy(
            src_ref=table, dst_ref=cells_all.at[me], send_sem=cell_send.at[step],
            recv_sem=cell_recv.at[me], device_id=to((me + step) % device_count),
            device_id_type=pl.DeviceIdType.MESH,
        )

    def cell_arrival(source):
        return pltpu.make_async_remote_copy(
            src_ref=table, dst_ref=cells_all.at[source], send_sem=cell_send.at[0],
            recv_sem=cell_recv.at[source], device_id=to((me + 1) % device_count),
            device_id_type=pl.DeviceIdType.MESH,
        )

    barrier = pltpu.get_barrier_semaphore()

    def greet(step, _):
        pl.semaphore_signal(
            barrier, inc=1, device_id=to((me + step) % device_count), device_id_type=pl.DeviceIdType.MESH
        )
        return 0

    lax.fori_loop(1, device_count, greet, 0)
    pl.semaphore_wait(barrier, device_count - 1)

    def send_cells(step, _):
        cell_copy(step).start()
        return 0

    lax.fori_loop(1, device_count, send_cells, 0)
    cells_all[me] = table[...]

    def rotate(cos_a, sin_a, cos_b, sin_b):
        return cos_a * cos_b - sin_a * sin_b, sin_a * cos_b + cos_a * sin_b

    def build_y(step, _):
        at = pl.ds(pl.multiple_of(step * INNER, INNER), INNER)
        row = pl.ds(side * (half // INNER) + step, 1)
        for parity in range(2):
            for part in range(half // 256):
                lanes = pl.ds(parity * half + part * 256, 256)
                out = pl.ds(part * 256, 256)
                cosine, sine = rotate(
                    ccos[row, lanes], csin[row, lanes], fcos[:INNER, lanes], fsin[:INNER, lanes]
                )
                ych[parity, at, out], ycl[parity, at, out] = split(cosine)
                ysh[parity, at, out], ysl[parity, at, out] = split(sine)
        return 0

    def build_x(step, high, low, pick):
        at = pl.ds(pl.multiple_of(step * INNER, INNER), INNER)
        row = pl.ds(step, 1)
        for parity in range(2):
            for part in range(half // 256):
                lanes = pl.ds(part * 256, 256)
                value = rotate(gcos[row, lanes], gsin[row, lanes], hcos[parity, :, lanes], hsin[parity, :, lanes])
                high[parity, at, lanes], low[parity, at, lanes] = split(value[pick])
        return 0

    lax.fori_loop(0, half // INNER, lambda s, c: build_x(s, xch, xcl, 0), 0)
    lax.fori_loop(0, half // INNER, build_y, 0)

    mine = pl.ds(pl.multiple_of(spot * LANES, LANES), LANES)
    coarse_rows = length // INNER
    for index, (fine_ref, coarse_ref) in enumerate(((fcos, ccos), (fsin, csin))):
        into = pl.ds(index * LANES, LANES)
        pad = jnp.zeros((LANES - FINE, LANES), f32)
        value = fine_ref[:, mine]
        high = value.astype(bf16).astype(f32)
        xf[into, :LANES] = jnp.concatenate([high, pad], 0).T.astype(bf16)
        xf[into, LANES:] = jnp.concatenate([value - high, pad], 0).T.astype(bf16)
        value = coarse_ref[:, mine]
        high = value.astype(bf16).astype(f32)
        xg[into, :] = jnp.concatenate([high, value - high], 0).T.astype(bf16)

    def take_cells(step, _):
        cell_arrival((me + step) % device_count).wait_recv()
        return 0

    lax.fori_loop(1, device_count, take_cells, 0)

    def slab_cells(index):
        block = jnp.concatenate([cells_all[2 * index], cells_all[2 * index + 1]], axis=1)
        return [block[i : i + 1, :] for i in range(7)]

    carry[...] = jnp.zeros_like(carry)

    def spread(index, _):
        row, col, wide, high, region, off_x, off_y = slab_cells(index)
        upper = index // halves
        window = jnp.floor(col * (1.0 / INNER))
        local = col - window * INNER
        near = overlap(row_iota(FINE, both) - local, off_x, wide).astype(bf16)
        gap = jnp.zeros((LANES - FINE, both), bf16)
        hot = jnp.where(row_iota(coarse_rows, both) == window, 1.0, 0.0).astype(bf16)
        fine_part = dot(xf[...], jnp.concatenate([near, gap, near, gap], 0))
        coarse_part = dot(xg[...], jnp.concatenate([hot, hot], 0))
        along = fine_part[:LANES] * coarse_part[:LANES] - fine_part[LANES:] * coarse_part[LANES:]
        waves = jnp.concatenate(split(along), 0)
        start = (index * slab_rows).astype(f32)
        flip = upper.astype(f32)
        ladder = row_iota(slab_rows, both)
        place = start + ladder + flip * (slab_rows - 1.0 - 2.0 * ladder)
        tall = overlap(place - row, off_y, high).astype(bf16)
        flip_next = ((index + 1) // halves).astype(f32)
        steps = row_iota(8, both)
        place = start + slab_rows + steps + flip_next * (7.0 - 2.0 * steps)
        above = overlap(place - row, off_y, high)
        masks = [jnp.where(region == g, 1.0, 0.0) for g in range(regions)]
        above = jnp.concatenate([above * mask for mask in masks], 0).astype(bf16)
        stack = jnp.concatenate([tall * mask.astype(bf16) for mask in masks] + [above], 0)
        result = dot(stack, waves, ((1,), (1,)))
        result = result[:, :LANES] + result[:, LANES:]
        tile = index + upper * (2 * halves - 1 - 2 * index)
        base = pl.multiple_of(tile * slab_rows, slab_rows)
        edge = pl.multiple_of(tile * slab_rows + upper * (slab_rows - 8), 8)
        for g in range(regions):
            lanes = pl.ds(g * LANES, LANES)
            draw[upper, pl.ds(base, slab_rows), lanes] = result[g * slab_rows : (g + 1) * slab_rows]
            draw[upper, pl.ds(edge, 8), lanes] += carry[g * 8 : (g + 1) * 8, :]
        carry[...] = result[regions * slab_rows :]
        return 0

    lax.fori_loop(0, slab_count, spread, 0)

    def fold(step, _):
        at = pl.ds(pl.multiple_of(step * 64, 64), 64)
        lower, upper = draw[0, at, :], draw[1, at, :]
        foh[0, at, :], fol[0, at, :] = split(lower + upper)
        foh[1, at, :], fol[1, at, :] = split(lower - upper)
        return 0

    lax.fori_loop(0, half // 64, fold, 0)

    step_size = math.pi / length
    energy_acc[...] = jnp.zeros_like(energy_acc)
    chunk = 256
    kx = 2 * ((spot % halves) * LANES + lax.broadcasted_iota(jnp.int32, (chunk, LANES), 1)) + spot // halves
    kx = kx.astype(f32)

    def transform(step, _):
        parity = step // (half // chunk)
        first = (step % (half // chunk)) * chunk
        at = pl.ds(pl.multiple_of(first, chunk), chunk)
        high, low = xch[parity, at, :], xcl[parity, at, :]
        spectrum = dot(high, foh[parity]) + (dot(high, fol[parity]) + dot(low, foh[parity]))
        ky = (2 * (first + lax.broadcasted_iota(jnp.int32, (chunk, LANES), 0)) + parity).astype(f32)
        squared = kx * kx + ky * ky
        at_anchor = squared == 0.0
        scale = jnp.where(kx == 0.0, 1.0 / length, 2.0 / length) * jnp.where(ky == 0.0, 1.0 / length, 2.0 / length)
        weight = jnp.where(
            at_anchor, 0.0, scale / (step_size * step_size * jnp.where(at_anchor, 1.0, squared))
        )
        weight_x = weight * (step_size * kx)
        weight_y = weight * (step_size * ky)
        energy = energy_acc[...]
        for g in range(regions):
            lanes = pl.ds(g * LANES, LANES)
            part = spectrum[:, g * LANES : (g + 1) * LANES]
            hxh[parity, at, lanes], hxl[parity, at, lanes] = split(part * weight_x)
            hyh[parity, at, lanes], hyl[parity, at, lanes] = split(part * weight_y)
            energy += fold_rows(part * part * weight)
        energy_acc[...] = energy
        return 0

    lax.fori_loop(0, 2 * (half // chunk), transform, 0)

    def data_copy(target, source, place):
        return pltpu.make_async_remote_copy(
            src_ref=send_buf.at[target], dst_ref=recv_buf.at[source], send_sem=data_send.at[target],
            recv_sem=data_recv.at[source], device_id=to(side * group + place), device_id_type=pl.DeviceIdType.MESH,
        )

    def scale_copy(target, source, place):
        return pltpu.make_async_remote_copy(
            src_ref=send_scale.at[target], dst_ref=recv_scale.at[source], send_sem=scale_send.at[target],
            recv_sem=scale_recv.at[source], device_id=to(side * group + place), device_id_type=pl.DeviceIdType.MESH,
        )

    tiles = group // 4

    def inverse(step, _):
        tile = (spot // 4 + step + 1) % tiles
        at = pl.ds(pl.multiple_of(tile * (4 * rows), 4 * rows), 4 * rows)
        for index, (th, tl, vh, vl) in enumerate(((ych, ycl, hxh, hxl), (ysh, ysl, hyh, hyl))):
            value = None
            for parity in range(2):
                high, low = th[parity, at, :], tl[parity, at, :]
                term = dot(high, vh[parity]) + (dot(high, vl[parity]) + dot(low, vh[parity]))
                value = term if value is None else value + term
            for part in range(4):
                block = value[part * rows : (part + 1) * rows]
                top = jnp.maximum(jnp.max(jnp.abs(block), axis=0, keepdims=True), 1e-30)
                code = jnp.round(block * (CODE_TOP / top)).astype(jnp.int32).astype(jnp.int16)
                send_buf[tile * 4 + part, index] = code
                send_scale[tile * 4 + part, pl.ds(index, 1), :] = top * (1.0 / CODE_TOP)
        for part in range(4):
            target = tile * 4 + part

            @pl.when(target != spot)
            def _():
                data_copy(target, spot, target).start()
                scale_copy(target, spot, target).start()

            @pl.when(target == spot)
            def _():
                recv_buf[spot] = send_buf[spot]
                recv_scale[spot] = send_scale[spot]

        return 0

    lax.fori_loop(0, tiles, inverse, 0)

    own = slab_cells(slab)
    under = slab_cells((slab + slab_count - 1) % slab_count)
    start = (slab * slab_rows + core * rows).astype(f32)
    for count, ref, (row, _, _, high, region, _, off_y) in ((rows, yown, own), (8, ybelow, under)):
        reach = overlap(start + row_iota(count, both) - row, off_y, high)
        for g in range(regions):
            ref[pl.ds(g * count, count), :] = jnp.where(region == g, reach, 0.0).astype(bf16)

    def columns(step, _):
        at = pl.ds(pl.multiple_of(step * 64, 64), 64)
        for part in range(2):
            spots = row_iota(64, both) + (step * 64 + part * half).astype(f32)
            for ref, (_, col, wide, _, _, off_x, _) in ((ych, own), (ycl, under)):
                ref[part, at, :] = overlap(spots - col, off_x, wide).astype(bf16)
        return 0

    lax.fori_loop(0, half // 64, columns, 0)
    excess_acc[...] = jnp.zeros_like(excess_acc)
    area_acc[...] = jnp.zeros_like(area_acc)

    def measure(step, _):
        part = step // (half // 256)
        at = pl.ds(pl.multiple_of((step % (half // 256)) * 256, 256), 256)
        density = dot(yown[...], ych[part, at, :], ((1,), (1,)))
        extra = dot(ybelow[...], ycl[part, at, :], ((1,), (1,)))
        excess, area = excess_acc[...], area_acc[...]
        for g in range(regions):
            block = density[g * rows : (g + 1) * rows]
            for piece in (block[:8] + extra[g * 8 : (g + 1) * 8], block[8:]):
                area += fold_rows(piece)
                excess += fold_rows(jnp.maximum(piece - 1.0, 0.0))
        excess_acc[...], area_acc[...] = excess, area
        return 0

    lax.fori_loop(0, length // 256, measure, 0)

    lane = lax.broadcasted_iota(jnp.int32, (8, LANES), 1)
    sums = jnp.where(lane == 0, jnp.sum(excess_acc[...]), 0.0)
    sums = jnp.where(lane == 1, jnp.sum(area_acc[...]), sums)
    sums = jnp.where(lane == 2, jnp.sum(energy_acc[...]) * (0.5 / (length * length)), sums)
    scal_out[...] = sums
    scal_in[me] = sums

    def scal_copy(step, source):
        return pltpu.make_async_remote_copy(
            src_ref=scal_out, dst_ref=scal_in.at[source], send_sem=scal_send.at[step],
            recv_sem=scal_recv.at[source], device_id=to((me + step) % device_count),
            device_id_type=pl.DeviceIdType.MESH,
        )

    def send_sums(step, _):
        scal_copy(step, me).start()
        return 0

    lax.fori_loop(1, device_count, send_sums, 0)
    lax.fori_loop(0, half // INNER, lambda s, c: build_x(s, ysh, ysl, 1), 0)

    def unpack(step, _):
        source = (spot + step) % group

        @pl.when(source != spot)
        def _():
            data_copy(source, source, source).wait_recv()
            scale_copy(source, source, source).wait_recv()

        across = source // 4
        lanes = pl.ds(pl.multiple_of((source % 4) * LANES, LANES), LANES)
        for index in range(2):
            factor = recv_scale[source, pl.ds(index, 1), :]
            value = recv_buf[source, index].astype(jnp.int32).astype(f32) * factor
            for g in range(regions):
                at = pl.ds(pl.multiple_of(across * (regions * rows) + g * rows, rows), rows)
                foh[index, at, lanes], fol[index, at, lanes] = split(value[:, g * LANES : (g + 1) * LANES])
        return 0

    lax.fori_loop(0, group, unpack, 0)

    high_rows = regions * rows
    mirror = LANES - 1 - lax.broadcasted_iota(jnp.int32, (high_rows, LANES), 1)
    wide = 256
    for index, (th, tl, out) in enumerate(((ysh, ysl, field_x), (xch, xcl, field_y))):

        def finish(step, _, index=index, th=th, tl=tl, out=out):
            at = pl.ds(pl.multiple_of(step * wide, wide), wide)
            sums = []
            for parity in range(2):
                total = None
                for block in range(2):
                    pick = pl.ds((parity * 2 + block) * high_rows, high_rows)
                    high, low = foh[index, pick, :], fol[index, pick, :]
                    depth = pl.ds(block * 512, 512)
                    left, right = th[parity, depth, at], tl[parity, depth, at]
                    term = dot(high, left) + (dot(high, right) + dot(low, left))
                    total = term if total is None else total + term
                sums.append(total)
            even, odd = sums
            straight = even + odd
            back = even - odd if index else odd - even
            rounded[index, :, at] = straight.astype(bf16)
            for g in range(regions):
                out[g, :, at] = straight[g * rows : (g + 1) * rows]
            for part in range(wide // LANES):
                tile = jnp.take_along_axis(
                    back[:, part * LANES : (part + 1) * LANES], mirror, axis=1, mode="promise_in_bounds"
                )
                far = pl.ds(pl.multiple_of(length - (part + 1) * LANES - step * wide, LANES), LANES)
                rounded[index, :, far] = tile.astype(bf16)
                for g in range(regions):
                    out[g, :, far] = tile[g * rows : (g + 1) * rows]
            return 0

        lax.fori_loop(0, half // wide, finish, 0)

    for index, out in enumerate((field_x, field_y)):
        low_rows = jnp.concatenate([out[g, :8, :] for g in range(regions)], 0).astype(bf16)
        total = dot(rounded[index, :, :half], ych[0]) + dot(rounded[index, :, half:], ych[1])
        extra = dot(low_rows[:, :half], ycl[0]) + dot(low_rows[:, half:], ycl[1])
        total = jnp.sum(total * yown[...].astype(f32), axis=0, keepdims=True)
        extra = jnp.sum(extra * ybelow[...].astype(f32), axis=0, keepdims=True)
        for part in range(2):
            part_own[part, pl.ds(index, 1), :] = total[:, part * cells : (part + 1) * cells]
            part_below[part, pl.ds(index, 1), :] = extra[:, part * cells : (part + 1) * cells]

    def sibling_copy():
        return pltpu.make_async_remote_copy(
            src_ref=part_own.at[1 - core], dst_ref=part_sib, send_sem=part_send.at[0],
            recv_sem=part_recv.at[0], device_id=(slab, 1 - core), device_id_type=pl.DeviceIdType.MESH,
        )

    def down_copy(part):
        return pltpu.make_async_remote_copy(
            src_ref=part_below.at[part], dst_ref=part_up, send_sem=part_send.at[1 + part],
            recv_sem=part_recv.at[1], device_id=(lax.max(slab - 1, 0), part),
            device_id_type=pl.DeviceIdType.MESH,
        )

    sibling_copy().start()

    @pl.when((core == 0) & (slab > 0))
    def _():
        down_copy(0).start()
        down_copy(1).start()

    def take_sums(step, _):
        scal_copy(step, (me + step) % device_count).wait_recv()
        return 0

    lax.fori_loop(1, device_count, take_sums, 0)
    total = scal_in[0]
    for source in range(1, device_count):
        total += scal_in[source]
    scalars[...] = total
    sibling_copy().wait_recv()
    force[...] = (part_own[core] + part_sib[...])[:2]

    @pl.when(slab < slab_count - 1)
    def _():
        down_copy(0).wait_recv()
        force[...] += part_up[:2, :]

    def drain(step, _):
        cell_copy(step).wait_send()
        scal_copy(step, me).wait_send()
        return 0

    lax.fori_loop(1, device_count, drain, 0)

    def drain_data(step, _):
        target = (spot + step) % group
        data_copy(target, spot, target).wait_send()
        scale_copy(target, spot, target).wait_send()
        return 0

    lax.fori_loop(1, group, drain_data, 0)
    sibling_copy().wait_send()

    @pl.when((core == 0) & (slab > 0))
    def _():
        down_copy(0).wait_send()
        down_copy(1).wait_send()


def fused_body(cell_row, cell_col, cell_width, cell_height, cell_region, cell_offset):
    slab_count = lax.axis_size("slab")
    length, regions = M, REGIONS
    cells = cell_row.shape[0]
    half, group = length // 2, slab_count
    device_count = 2 * slab_count
    rows = length // device_count
    f32, bf16 = jnp.float32, jnp.bfloat16
    table = jnp.concatenate(
        [
            jnp.stack([cell_row, cell_col, cell_width, cell_height, cell_region]).astype(f32),
            cell_offset,
            jnp.zeros((1, cells), f32),
        ]
    )
    consts = [jnp.asarray(t) for t in small_tables(length)]
    vmem = pltpu.VMEM
    basis = vmem((2, half, half), bf16)
    panel = vmem((2, half, regions * LANES), bf16)
    sems = pltpu.SemaphoreType.DMA
    scratch = (
        [vmem((device_count, 8, cells), f32)]
        + [basis] * 6
        + [vmem((2, half, regions * LANES), f32)]
        + [panel] * 6
        + [
            vmem((group, 2, rows, regions * LANES), jnp.int16),
            vmem((group, 2, regions * LANES), f32),
            vmem((group, 2, rows, regions * LANES), jnp.int16),
            vmem((group, 2, regions * LANES), f32),
            vmem((2, regions * rows, length), bf16),
            vmem((2 * LANES, 2 * LANES), bf16),
            vmem((2 * LANES, 2 * (length // INNER)), bf16),
            vmem((8 * regions, LANES), f32),
            vmem((regions * rows, 2 * cells), bf16),
            vmem((8 * regions, 2 * cells), bf16),
            vmem((8, LANES), f32),
            vmem((8, 256), f32),
            vmem((8, 256), f32),
            vmem((8, LANES), f32),
            vmem((device_count, 8, LANES), f32),
            vmem((2, 8, cells), f32),
            vmem((2, 8, cells), f32),
            vmem((8, cells), f32),
            vmem((8, cells), f32),
            sems((device_count,)),
            sems((device_count,)),
            sems((group,)),
            sems((group,)),
            sems((group,)),
            sems((group,)),
            sems((device_count,)),
            sems((device_count,)),
            sems((3,)),
            sems((2,)),
        ]
    )
    whole = pl.BlockSpec(memory_space=vmem)
    field = jax.ShapeDtypeStruct((regions, rows, length), f32)
    field_x, field_y, force, scalars = pl.pallas_call(
        functools.partial(fused_kernel, slab_count, length, cells, regions),
        out_shape=(
            field,
            field,
            jax.ShapeDtypeStruct((2, cells), f32),
            jax.ShapeDtypeStruct((8, LANES), f32),
        ),
        in_specs=[whole] * (1 + len(consts)),
        out_specs=(whole,) * 4,
        scratch_shapes=scratch,
        compiler_params=pltpu.CompilerParams(
            collective_id=0, has_side_effects=True, vmem_limit_bytes=67043328
        ),
    )(table, *consts)
    return field_x, field_y, force, scalars[0, 2], scalars[0, 0] / scalars[0, 1]


def fits(mesh):
    slab_count = mesh.shape["slab"]
    return mesh.shape["cell"] == 2 and slab_count % 8 == 0 and M == slab_count * LANES


def solution(mesh):
    return jax.shard_map(
        fused_body if fits(mesh) else body,
        mesh=mesh,
        in_specs=(
            P(("slab", "cell")),
            P(("slab", "cell")),
            P(("slab", "cell")),
            P(("slab", "cell")),
            P(("slab", "cell")),
            P(None, ("slab", "cell")),
        ),
        out_specs=(
            P(None, ("slab", "cell"), None),
            P(None, ("slab", "cell"), None),
            P(None, ("slab", "cell")),
            P(),
            P(),
        ),
        check_vma=False,
    )
```

profile of v0, /device:TPU:13, one launch (start us, length us, event | category | flops | bytes accessed | tf_op | source)
XLA Modules:
  0.0 115.5 jit_solution(15242023980070234929)
XLA Ops:
  0.6 0.8 stack.23
  1.4 0.1 pad.2.clone
  1.5 1.4 %maximum_maximum_fusion.table = f32[8,512]{1,0:T(8,128)} fusion(f32[2,512]{1,0:T(2,128)} %param.19, f32[5,512]{1,0:T(8,128)S(1)} %convert_element_type.3, f32[8]{0:T(128)S(1)} %pad.2.clone), kind=kLoop, calls=%fused_computation | loop fusion | flops 8192 | bytes 30752 | tf_op jit(solution)/shard_map/concatenate | solution.py:668
  2.9 103.5 %shard_map.173 = (f32[4,64,2048]{2,1,0:T(8,128)}, f32[4,64,2048]{2,1,0:T(8,128)}, f32[2,512]{1,0:T(2,128)}, f32[8,128]{1,0:T(8,128)}) custom-call(f32[8,512]{1,0:T(8,128)} %maximum_maximum_fusion.table, f32[64,2048]{1,0:T(8,128)} %constant.18.clone.ccos, f32[64,2048]{1,0:T(8,128)} %constant.19.clone.csin, f32[48,2048]{1,0:T(8,128)} %constant.20.clone.fcos, ...), custom_call_target="tpu_custom_call" | custom-call | tf_op jit(solution)/shard_map/pallas_call | solution.py:719
  106.4 1.4 %fusion = (f32[1,1]{1,0:T(1,128)}, f32[1,1]{1,0:T(1,128)}, f32[1,1]{1,0:T(1,128)}) fusion(f32[8,128]{1,0:T(8,128)} %get-tuple-element.12), kind=kLoop, calls=%fused_computation.1 | loop fusion | bytes 24 | tf_op jit(solution)/shard_map/slice | solution.py:734
  109.1 0.0 copy-start
  109.1 3.3 %copy.22 = f32[4,64,2048]{2,1,0:T(8,128)} copy(f32[4,64,2048]{2,1,0:T(8,128)} %get-tuple-element.21) | data formatting | bytes 4194304
  112.4 0.0 copy-done
  112.4 0.0 copy-start.1
  112.4 1.3 %copy.23 = f32[4,64,2048]{2,1,0:T(8,128)} copy(f32[4,64,2048]{2,1,0:T(8,128)S(1)} %copy-done) | data formatting | bytes 4194304
  113.7 0.0 copy-done.1
  113.7 0.6 copy.24
  (1 shorter events, 0.0 us)
Async XLA Ops:
  109.1 3.3 %copy-start = (f32[4,64,2048]{2,1,0:T(8,128)S(1)}, f32[4,64,2048]{2,1,0:T(8,128)}, u32[]{:S(2)}) copy-start(f32[4,64,2048]{2,1,0:T(8,128)} %get-tuple-element.22) | copy-start | bytes 6291460
  112.4 1.3 %copy-start.1 = (f32[2,512]{1,0:T(2,128)S(1)}, f32[2,512]{1,0:T(2,128)}, u32[]{:S(2)}) copy-start(f32[2,512]{1,0:T(2,128)} %get-tuple-element.23) | copy-start | bytes 12292
where the time goes:
time: 116 us; the launch traced here: 115 us
  Pallas kernels  104 us (90%)
  local copies, waits for them, and re-layouts  7.43 us (6%)
  between operations  3.13 us (3%)
  other arithmetic  1.37 us (1%)
    pallas_call x1, Pallas kernels, fused_body(): pl.pallas_call(functools.partial(fused_kernel, slab_count, length, cells,...  104 us
    unnamed x7, local copies, waits for them, and re-layouts  5.2 us

commit v1 on v0

--- a/solution.py
+++ b/solution.py
@@ -237,13 +237,13 @@
 
 def fused_kernel(
     slab_count, length, cells, regions,
-    table, ccos, csin, fcos, fsin, gcos, gsin, hcos, hsin,
-    field_x, field_y, force, scalars,
-    cells_all, xch, xcl, ych, ycl, ysh, ysl, draw, foh, fol, hxh, hxl, hyh, hyl,
+    cell_row, cell_col, cell_width, cell_height, cell_region, cell_offset, ccos, csin, fcos, fsin, gcos, gsin, hcos, hsin,
+    out_x, out_y, force, scalars,
+    table, field_x, field_y, cells_all, xch, xcl, ych, ycl, ysh, ysl, draw, foh, fol, hxh, hxl, hyh, hyl,
     send_buf, send_scale, recv_buf, recv_scale, rounded, xf, xg, carry, yown, ybelow,
     energy_acc, excess_acc, area_acc, scal_out, scal_in, part_own, part_below, part_sib, part_up,
     cell_send, cell_recv, data_send, data_recv, scale_send, scale_recv,
-    scal_send, scal_recv, part_send, part_recv,
+    scal_send, scal_recv, part_send, part_recv, out_sem,
 ):
     half = length // 2
     halves = slab_count // 2
@@ -262,10 +262,13 @@
     def to(index):
         return (index // 2, index % 2)
 
+    def neighbour(step):
+        return ((slab + step // 2) % slab_count, (core + step) % 2)
+
     def cell_copy(step):
         return pltpu.make_async_remote_copy(
             src_ref=table, dst_ref=cells_all.at[me], send_sem=cell_send.at[step],
-            recv_sem=cell_recv.at[me], device_id=to((me + step) % device_count),
+            recv_sem=cell_recv.at[me], device_id=neighbour(step),
             device_id_type=pl.DeviceIdType.MESH,
         )
 
@@ -285,6 +288,10 @@
         return 0
 
     lax.fori_loop(1, device_count, greet, 0)
+    for index, ref in enumerate((cell_row, cell_col, cell_width, cell_height, cell_region)):
+        table[pl.ds(index, 1), :] = ref[...].reshape(1, cells).astype(f32)
+    table[5:7, :] = cell_offset[...]
+    table[7:8, :] = jnp.zeros((1, cells), f32)
     pl.semaphore_wait(barrier, device_count - 1)
 
     def send_cells(step, _):
@@ -337,19 +344,18 @@
         high = value.astype(bf16).astype(f32)
         xg[into, :] = jnp.concatenate([high, value - high], 0).T.astype(bf16)
 
-    def take_cells(step, _):
-        cell_arrival((me + step) % device_count).wait_recv()
-        return 0
-
-    lax.fori_loop(1, device_count, take_cells, 0)
-
     def slab_cells(index):
         block = jnp.concatenate([cells_all[2 * index], cells_all[2 * index + 1]], axis=1)
         return [block[i : i + 1, :] for i in range(7)]
 
-    carry[...] = jnp.zeros_like(carry)
-
-    def spread(index, _):
+    def spread(step, _):
+        index = (slab + slab_count - step) % slab_count
+        for part in range(2):
+
+            @pl.when(2 * index + part != me)
+            def _():
+                cell_arrival(2 * index + part).wait_recv()
+
         row, col, wide, high, region, off_x, off_y = slab_cells(index)
         upper = index // halves
         window = jnp.floor(col * (1.0 / INNER))
@@ -377,15 +383,24 @@
         result = result[:, :LANES] + result[:, LANES:]
         tile = index + upper * (2 * halves - 1 - 2 * index)
         base = pl.multiple_of(tile * slab_rows, slab_rows)
+        for g in range(regions):
+            lanes = pl.ds(g * LANES, LANES)
+            draw[upper, pl.ds(base, slab_rows), lanes] = result[g * slab_rows : (g + 1) * slab_rows]
+        carry[index] = result[regions * slab_rows :]
+        return 0
+
+    lax.fori_loop(0, slab_count, spread, 0)
+
+    def hand_up(index, _):
+        upper = index // halves
+        tile = index + upper * (2 * halves - 1 - 2 * index)
         edge = pl.multiple_of(tile * slab_rows + upper * (slab_rows - 8), 8)
         for g in range(regions):
             lanes = pl.ds(g * LANES, LANES)
-            draw[upper, pl.ds(base, slab_rows), lanes] = result[g * slab_rows : (g + 1) * slab_rows]
-            draw[upper, pl.ds(edge, 8), lanes] += carry[g * 8 : (g + 1) * 8, :]
-        carry[...] = result[regions * slab_rows :]
-        return 0
-
-    lax.fori_loop(0, slab_count, spread, 0)
+            draw[upper, pl.ds(edge, 8), lanes] += carry[index - 1, g * 8 : (g + 1) * 8, :]
+        return 0
+
+    lax.fori_loop(1, slab_count, hand_up, 0)
 
     def fold(step, _):
         at = pl.ds(pl.multiple_of(step * 64, 64), 64)
@@ -429,51 +444,55 @@
 
     lax.fori_loop(0, 2 * (half // chunk), transform, 0)
 
-    def data_copy(target, source, place):
+    def data_copy(index, target, source, place):
         return pltpu.make_async_remote_copy(
-            src_ref=send_buf.at[target], dst_ref=recv_buf.at[source], send_sem=data_send.at[target],
-            recv_sem=data_recv.at[source], device_id=to(side * group + place), device_id_type=pl.DeviceIdType.MESH,
-        )
-
-    def scale_copy(target, source, place):
+            src_ref=send_buf.at[index, target], dst_ref=recv_buf.at[index, source],
+            send_sem=data_send.at[index, target], recv_sem=data_recv.at[index, source],
+            device_id=to(side * group + place), device_id_type=pl.DeviceIdType.MESH,
+        )
+
+    def scale_copy(index, target, source, place):
         return pltpu.make_async_remote_copy(
-            src_ref=send_scale.at[target], dst_ref=recv_scale.at[source], send_sem=scale_send.at[target],
-            recv_sem=scale_recv.at[source], device_id=to(side * group + place), device_id_type=pl.DeviceIdType.MESH,
+            src_ref=send_scale.at[index, target], dst_ref=recv_scale.at[index, source],
+            send_sem=scale_send.at[index, target], recv_sem=scale_recv.at[index, source],
+            device_id=to(side * group + place), device_id_type=pl.DeviceIdType.MESH,
         )
 
     tiles = group // 4
 
-    def inverse(step, _):
+    def inverse(step, _, index, th, tl, vh, vl):
         tile = (spot // 4 + step + 1) % tiles
         at = pl.ds(pl.multiple_of(tile * (4 * rows), 4 * rows), 4 * rows)
-        for index, (th, tl, vh, vl) in enumerate(((ych, ycl, hxh, hxl), (ysh, ysl, hyh, hyl))):
-            value = None
-            for parity in range(2):
-                high, low = th[parity, at, :], tl[parity, at, :]
-                term = dot(high, vh[parity]) + (dot(high, vl[parity]) + dot(low, vh[parity]))
-                value = term if value is None else value + term
-            for part in range(4):
-                block = value[part * rows : (part + 1) * rows]
-                top = jnp.maximum(jnp.max(jnp.abs(block), axis=0, keepdims=True), 1e-30)
-                code = jnp.round(block * (CODE_TOP / top)).astype(jnp.int32).astype(jnp.int16)
-                send_buf[tile * 4 + part, index] = code
-                send_scale[tile * 4 + part, pl.ds(index, 1), :] = top * (1.0 / CODE_TOP)
+        value = None
+        for parity in range(2):
+            high, low = th[parity, at, :], tl[parity, at, :]
+            term = dot(high, vh[parity]) + (dot(high, vl[parity]) + dot(low, vh[parity]))
+            value = term if value is None else value + term
+        for part in range(4):
+            block = value[part * rows : (part + 1) * rows]
+            top = jnp.maximum(jnp.max(jnp.abs(block), axis=0, keepdims=True), 1e-30)
+            code = jnp.round(block * (CODE_TOP / top)).astype(jnp.int32).astype(jnp.int16)
+            send_buf[index, tile * 4 + part] = code
+            send_scale[index, tile * 4 + part] = jnp.broadcast_to(top * (1.0 / CODE_TOP), (2, regions * LANES))
         for part in range(4):
             target = tile * 4 + part
 
             @pl.when(target != spot)
             def _():
-                data_copy(target, spot, target).start()
-                scale_copy(target, spot, target).start()
+                data_copy(index, target, spot, target).start()
+                scale_copy(index, target, spot, target).start()
 
             @pl.when(target == spot)
             def _():
-                recv_buf[spot] = send_buf[spot]
-                recv_scale[spot] = send_scale[spot]
-
-        return 0
-
-    lax.fori_loop(0, tiles, inverse, 0)
+                recv_buf[index, spot] = send_buf[index, spot]
+                recv_scale[index, spot] = send_scale[index, spot]
+
+        return 0
+
+    for index, (th, tl, vh, vl) in enumerate(((ych, ycl, hxh, hxl), (ysh, ysl, hyh, hyl))):
+        lax.fori_loop(
+            0, tiles, functools.partial(inverse, index=index, th=th, tl=tl, vh=vh, vl=vl), 0
+        )
 
     own = slab_cells(slab)
     under = slab_cells((slab + slab_count - 1) % slab_count)
@@ -532,65 +551,63 @@
     lax.fori_loop(1, device_count, send_sums, 0)
     lax.fori_loop(0, half // INNER, lambda s, c: build_x(s, ysh, ysl, 1), 0)
 
-    def unpack(step, _):
+    def unpack(step, _, index):
         source = (spot + step) % group
 
         @pl.when(source != spot)
         def _():
-            data_copy(source, source, source).wait_recv()
-            scale_copy(source, source, source).wait_recv()
+            data_copy(index, source, source, source).wait_recv()
+            scale_copy(index, source, source, source).wait_recv()
 
         across = source // 4
         lanes = pl.ds(pl.multiple_of((source % 4) * LANES, LANES), LANES)
-        for index in range(2):
-            factor = recv_scale[source, pl.ds(index, 1), :]
-            value = recv_buf[source, index].astype(jnp.int32).astype(f32) * factor
-            for g in range(regions):
-                at = pl.ds(pl.multiple_of(across * (regions * rows) + g * rows, rows), rows)
-                foh[index, at, lanes], fol[index, at, lanes] = split(value[:, g * LANES : (g + 1) * LANES])
-        return 0
-
-    lax.fori_loop(0, group, unpack, 0)
+        value = recv_buf[index, source].astype(jnp.int32).astype(f32) * recv_scale[index, source, :1, :]
+        for g in range(regions):
+            at = pl.ds(pl.multiple_of(across * (regions * rows) + g * rows, rows), rows)
+            foh[index, at, lanes], fol[index, at, lanes] = split(value[:, g * LANES : (g + 1) * LANES])
+        return 0
 
     high_rows = regions * rows
     mirror = LANES - 1 - lax.broadcasted_iota(jnp.int32, (high_rows, LANES), 1)
     wide = 256
-    for index, (th, tl, out) in enumerate(((ysh, ysl, field_x), (xch, xcl, field_y))):
-
-        def finish(step, _, index=index, th=th, tl=tl, out=out):
-            at = pl.ds(pl.multiple_of(step * wide, wide), wide)
-            sums = []
-            for parity in range(2):
-                total = None
-                for block in range(2):
-                    pick = pl.ds((parity * 2 + block) * high_rows, high_rows)
-                    high, low = foh[index, pick, :], fol[index, pick, :]
-                    depth = pl.ds(block * 512, 512)
-                    left, right = th[parity, depth, at], tl[parity, depth, at]
-                    term = dot(high, left) + (dot(high, right) + dot(low, left))
-                    total = term if total is None else total + term
-                sums.append(total)
-            even, odd = sums
-            straight = even + odd
-            back = even - odd if index else odd - even
-            rounded[index, :, at] = straight.astype(bf16)
+
+    def finish(step, _, index, th, tl, out):
+        at = pl.ds(pl.multiple_of(step * wide, wide), wide)
+        sums = []
+        for parity in range(2):
+            total = None
+            for block in range(2):
+                pick = pl.ds((parity * 2 + block) * high_rows, high_rows)
+                high, low = foh[index, pick, :], fol[index, pick, :]
+                depth = pl.ds(block * 512, 512)
+                left, right = th[parity, depth, at], tl[parity, depth, at]
+                term = dot(high, left) + (dot(high, right) + dot(low, left))
+                total = term if total is None else total + term
+            sums.append(total)
+        even, odd = sums
+        straight = even + odd
+        back = even - odd if index else odd - even
+        rounded[:, at] = straight.astype(bf16)
+        for g in range(regions):
+            out[g, :, at] = straight[g * rows : (g + 1) * rows]
+        for part in range(wide // LANES):
+            tile = jnp.take_along_axis(
+                back[:, part * LANES : (part + 1) * LANES], mirror, axis=1, mode="promise_in_bounds"
+            )
+            far = pl.ds(pl.multiple_of(length - (part + 1) * LANES - step * wide, LANES), LANES)
+            rounded[:, far] = tile.astype(bf16)
             for g in range(regions):
-                out[g, :, at] = straight[g * rows : (g + 1) * rows]
-            for part in range(wide // LANES):
-                tile = jnp.take_along_axis(
-                    back[:, part * LANES : (part + 1) * LANES], mirror, axis=1, mode="promise_in_bounds"
-                )
-                far = pl.ds(pl.multiple_of(length - (part + 1) * LANES - step * wide, LANES), LANES)
-                rounded[index, :, far] = tile.astype(bf16)
-                for g in range(regions):
-                    out[g, :, far] = tile[g * rows : (g + 1) * rows]
-            return 0
-
-        lax.fori_loop(0, half // wide, finish, 0)
-
-    for index, out in enumerate((field_x, field_y)):
+                out[g, :, far] = tile[g * rows : (g + 1) * rows]
+        return 0
+
+    leaving = []
+    for index, (th, tl, out, leave) in enumerate(((ysh, ysl, field_x, out_x), (xch, xcl, field_y, out_y))):
+        lax.fori_loop(0, group, functools.partial(unpack, index=index), 0)
+        lax.fori_loop(0, half // wide, functools.partial(finish, index=index, th=th, tl=tl, out=out), 0)
+        leaving.append(pltpu.make_async_copy(out, leave, out_sem.at[index]))
+        leaving[-1].start()
         low_rows = jnp.concatenate([out[g, :8, :] for g in range(regions)], 0).astype(bf16)
-        total = dot(rounded[index, :, :half], ych[0]) + dot(rounded[index, :, half:], ych[1])
+        total = dot(rounded[:, :half], ych[0]) + dot(rounded[:, half:], ych[1])
         extra = dot(low_rows[:, :half], ycl[0]) + dot(low_rows[:, half:], ycl[1])
         total = jnp.sum(total * yown[...].astype(f32), axis=0, keepdims=True)
         extra = jnp.sum(extra * ybelow[...].astype(f32), axis=0, keepdims=True)
@@ -626,7 +643,7 @@
     total = scal_in[0]
     for source in range(1, device_count):
         total += scal_in[source]
-    scalars[...] = total
+    scalars[...] = jnp.where(lane == 3, total[:, :1] / total[:, 1:2], total)
     sibling_copy().wait_recv()
     force[...] = (part_own[core] + part_sib[...])[:2]
 
@@ -644,8 +661,9 @@
 
     def drain_data(step, _):
         target = (spot + step) % group
-        data_copy(target, spot, target).wait_send()
-        scale_copy(target, spot, target).wait_send()
+        for index in range(2):
+            data_copy(index, target, spot, target).wait_send()
+            scale_copy(index, target, spot, target).wait_send()
         return 0
 
     lax.fori_loop(1, group, drain_data, 0)
@@ -655,6 +673,17 @@
     def _():
         down_copy(0).wait_send()
         down_copy(1).wait_send()
+
+    for copy in leaving:
+        copy.wait()
+
+
+def hand_out(in_x, in_y, in_force, in_scalars, out_x, out_y, force, energy, overflow):
+    out_x[...] = in_x[...]
+    out_y[...] = in_y[...]
+    force[...] = in_force[...]
+    energy[0, 0] = in_scalars[0, 2]
+    overflow[0, 0] = in_scalars[0, 3]
 
 
 def fused_body(cell_row, cell_col, cell_width, cell_height, cell_region, cell_offset):
@@ -665,32 +694,27 @@
     device_count = 2 * slab_count
     rows = length // device_count
     f32, bf16 = jnp.float32, jnp.bfloat16
-    table = jnp.concatenate(
-        [
-            jnp.stack([cell_row, cell_col, cell_width, cell_height, cell_region]).astype(f32),
-            cell_offset,
-            jnp.zeros((1, cells), f32),
-        ]
-    )
     consts = [jnp.asarray(t) for t in small_tables(length)]
     vmem = pltpu.VMEM
     basis = vmem((2, half, half), bf16)
     panel = vmem((2, half, regions * LANES), bf16)
     sems = pltpu.SemaphoreType.DMA
     scratch = (
-        [vmem((device_count, 8, cells), f32)]
+        [vmem((8, cells), f32)]
+        + [vmem((regions, rows, length), f32)] * 2
+        + [vmem((device_count, 8, cells), f32)]
         + [basis] * 6
         + [vmem((2, half, regions * LANES), f32)]
         + [panel] * 6
         + [
-            vmem((group, 2, rows, regions * LANES), jnp.int16),
-            vmem((group, 2, regions * LANES), f32),
-            vmem((group, 2, rows, regions * LANES), jnp.int16),
-            vmem((group, 2, regions * LANES), f32),
-            vmem((2, regions * rows, length), bf16),
+            vmem((2, group, rows, regions * LANES), jnp.int16),
+            vmem((2, group, 2, regions * LANES), f32),
+            vmem((2, group, rows, regions * LANES), jnp.int16),
+            vmem((2, group, 2, regions * LANES), f32),
+            vmem((regions * rows, length), bf16),
             vmem((2 * LANES, 2 * LANES), bf16),
             vmem((2 * LANES, 2 * (length // INNER)), bf16),
-            vmem((8 * regions, LANES), f32),
+            vmem((slab_count, 8 * regions, LANES), f32),
             vmem((regions * rows, 2 * cells), bf16),
             vmem((8 * regions, 2 * cells), bf16),
             vmem((8, LANES), f32),
@@ -704,17 +728,19 @@
             vmem((8, cells), f32),
             sems((device_count,)),
             sems((device_count,)),
-            sems((group,)),
-            sems((group,)),
-            sems((group,)),
-            sems((group,)),
+            sems((2, group)),
+            sems((2, group)),
+            sems((2, group)),
+            sems((2, group)),
             sems((device_count,)),
             sems((device_count,)),
             sems((3,)),
             sems((2,)),
+            sems((2,)),
         ]
     )
     whole = pl.BlockSpec(memory_space=vmem)
+    anywhere = pl.BlockSpec(memory_space=pl.ANY)
     field = jax.ShapeDtypeStruct((regions, rows, length), f32)
     field_x, field_y, force, scalars = pl.pallas_call(
         functools.partial(fused_kernel, slab_count, length, cells, regions),
@@ -724,14 +750,25 @@
             jax.ShapeDtypeStruct((2, cells), f32),
             jax.ShapeDtypeStruct((8, LANES), f32),
         ),
-        in_specs=[whole] * (1 + len(consts)),
-        out_specs=(whole,) * 4,
+        in_specs=[whole] * (6 + len(consts)),
+        out_specs=(anywhere, anywhere, whole, whole),
         scratch_shapes=scratch,
         compiler_params=pltpu.CompilerParams(
             collective_id=0, has_side_effects=True, vmem_limit_bytes=67043328
         ),
-    )(table, *consts)
-    return field_x, field_y, force, scalars[0, 2], scalars[0, 0] / scalars[0, 1]
+    )(cell_row, cell_col, cell_width, cell_height, cell_region, cell_offset, *consts)
+    block = pl.BlockSpec((1, rows, length), lambda g: (g, 0, 0))
+    small = pl.BlockSpec((2, cells), lambda g: (0, 0))
+    number = pl.BlockSpec((1, 1), lambda g: (0, 0), memory_space=pltpu.SMEM)
+    single = jax.ShapeDtypeStruct((1, 1), f32)
+    field_x, field_y, force, energy, overflow = pl.pallas_call(
+        hand_out,
+        grid=(regions,),
+        out_shape=(field, field, jax.ShapeDtypeStruct((2, cells), f32), single, single),
+        in_specs=[block, block, small, pl.BlockSpec((8, LANES), lambda g: (0, 0), memory_space=pltpu.SMEM)],
+        out_specs=(block, block, small, number, number),
+    )(field_x, field_y, force, scalars)
+    return field_x, field_y, force, energy.reshape(()), overflow.reshape(())
 
 
 def fits(mesh):

time: 116 us -> 92.3 us (0.80)
  Pallas kernels: 104 us -> 90.3 us
  local copies, waits for them, and re-layouts: 7.43 us -> 0 us
  between operations: 3.13 us -> 0.64 us
  other arithmetic: 1.37 us -> 0 us
    pallas_call x1, Pallas kernels: 104 us -> 85.6 us  [fused_body(): pl.pallas_call(functools.partial(fused_kernel, slab_count, length, cells,...]
    unnamed x7 -> x0, local copies, waits for them, and re-layouts: 5.2 us -> none
    pallas_call x0 -> x1, Pallas kernels: none -> 4.74 us  [fused_body(): pl.pallas_call(hand_out, grid=(regions,), out_shape=(field, field, jax.Sh...]
    slice x1 -> x0, local copies, waits for them, and re-layouts: 1.38 us -> none  [fused_body(): scalars[0, 1]]
    concatenate x1 -> x0, other arithmetic: 1.36 us -> none  [fused_body(): jnp.concatenate([jnp.stack([cell_row, cell_col, cell_width, cell_height,...]
where the time goes in v1:
time: 92.3 us; the launch traced here: 90.9 us
  Pallas kernels  90.3 us (98%)
    pallas_call x1, Pallas kernels, fused_body(): pl.pallas_call(functools.partial(fused_kernel, slab_count, length, cells,...  85.6 us
    pallas_call x1, Pallas kernels, fused_body(): pl.pallas_call(hand_out, grid=(regions,), out_shape=(field, field, jax.Sh...  4.74 us

profile of v1, /device:TPU:13, one launch (start us, length us, event | category | flops | bytes accessed | tf_op | source)
XLA Modules:
  0.0 90.9 jit_solution(11413102181112680870)
XLA Ops:
  0.6 85.6 %shard_map.173 = (f32[4,64,2048]{2,1,0:T(8,128)}, f32[4,64,2048]{2,1,0:T(8,128)}, f32[2,512]{1,0:T(2,128)}, f32[8,128]{1,0:T(8,128)}) custom-call(s32[512]{0:T(512)} %cell_row.1, s32[512]{0:T(512)} %cell_col.1, s32[512]{0:T(512)} %cell_width.1, s32[512]{0:T(512)} %cell_height.1, s32[512]{0:T(512)} %cell_region.1, f32[2,512]{1,0:T(2,128)} %cell_offset.1, ...), custom_call_target="tpu_custom_call" | custom-call | tf_op jit(solution)/shard_map/pallas_call | solution.py:745
  86.2 4.7 %shard_map.174 = (f32[4,64,2048]{2,1,0:T(8,128)}, f32[4,64,2048]{2,1,0:T(8,128)}, f32[2,512]{1,0:T(2,128)}, f32[1,1]{1,0:T(1,128)}, f32[1,1]{1,0:T(1,128)}) custom-call(f32[4,64,2048]{2,1,0:T(8,128)} %get-tuple-element.14.in_x, f32[4,64,2048]{2,1,0:T(8,128)} %get-tuple-element.15.in_y, f32[2,512]{1,0:T(2,128)} %get-tuple-element.16.in_force, ...), custom_call_target="tpu_custom_call" | custom-call | tf_op jit(solution)/shard_map/pallas_call | solution.py:764

commit v2 on v1

--- a/solution.py
+++ b/solution.py
@@ -237,13 +237,14 @@
 
 def fused_kernel(
     slab_count, length, cells, regions,
-    cell_row, cell_col, cell_width, cell_height, cell_region, cell_offset, ccos, csin, fcos, fsin, gcos, gsin, hcos, hsin,
+    cell_row, cell_col, cell_width, cell_height, cell_region, cell_offset,
+    src_0, src_1, src_2, src_3, src_4, src_5, src_6, src_7,
     out_x, out_y, force, scalars,
-    table, field_x, field_y, cells_all, xch, xcl, ych, ycl, ysh, ysl, draw, foh, fol, hxh, hxl, hyh, hyl,
+    ccos, csin, fcos, fsin, gcos, gsin, hcos, hsin, table, field_x, field_y, cells_all, xch, xcl, ych, ycl, ysh, ysl, draw, foh, fol, hxh, hxl, hyh, hyl,
     send_buf, send_scale, recv_buf, recv_scale, rounded, xf, xg, carry, yown, ybelow,
     energy_acc, excess_acc, area_acc, scal_out, scal_in, part_own, part_below, part_sib, part_up,
     cell_send, cell_recv, data_send, data_recv, scale_send, scale_recv,
-    scal_send, scal_recv, part_send, part_recv, out_sem,
+    scal_send, scal_recv, part_send, part_recv, out_sem, trig_sem,
 ):
     half = length // 2
     halves = slab_count // 2
@@ -279,6 +280,17 @@
             device_id_type=pl.DeviceIdType.MESH,
         )
 
+    tables = [
+        pltpu.make_async_copy(source, target, trig_sem.at[index])
+        for index, (source, target) in enumerate(
+            zip(
+                (src_0, src_1, src_2, src_3, src_4, src_5, src_6, src_7),
+                (ccos, csin, fcos, fsin, gcos, gsin, hcos, hsin),
+            )
+        )
+    ]
+    for copy in tables:
+        copy.start()
     barrier = pltpu.get_barrier_semaphore()
 
     def greet(step, _):
@@ -300,6 +312,8 @@
 
     lax.fori_loop(1, device_count, send_cells, 0)
     cells_all[me] = table[...]
+    for copy in tables:
+        copy.wait()
 
     def rotate(cos_a, sin_a, cos_b, sin_b):
         return cos_a * cos_b - sin_a * sin_b, sin_a * cos_b + cos_a * sin_b
@@ -349,13 +363,19 @@
         return [block[i : i + 1, :] for i in range(7)]
 
     def spread(step, _):
-        index = (slab + slab_count - step) % slab_count
-        for part in range(2):
-
-            @pl.when(2 * index + part != me)
-            def _():
-                cell_arrival(2 * index + part).wait_recv()
-
+        pair = [(slab + slab_count - 2 * step - back) % slab_count for back in range(2)]
+        for index in pair:
+            for part in range(2):
+
+                @pl.when(2 * index + part != me)
+                def _(source=2 * index + part):
+                    cell_arrival(source).wait_recv()
+
+        for index in pair:
+            spread_slab(index)
+        return 0
+
+    def spread_slab(index):
         row, col, wide, high, region, off_x, off_y = slab_cells(index)
         upper = index // halves
         window = jnp.floor(col * (1.0 / INNER))
@@ -387,9 +407,8 @@
             lanes = pl.ds(g * LANES, LANES)
             draw[upper, pl.ds(base, slab_rows), lanes] = result[g * slab_rows : (g + 1) * slab_rows]
         carry[index] = result[regions * slab_rows :]
-        return 0
-
-    lax.fori_loop(0, slab_count, spread, 0)
+
+    lax.fori_loop(0, slab_count // 2, spread, 0)
 
     def hand_up(index, _):
         upper = index // halves
@@ -413,7 +432,7 @@
 
     step_size = math.pi / length
     energy_acc[...] = jnp.zeros_like(energy_acc)
-    chunk = 256
+    chunk = 512
     kx = 2 * ((spot % halves) * LANES + lax.broadcasted_iota(jnp.int32, (chunk, LANES), 1)) + spot // halves
     kx = kx.astype(f32)
 
@@ -700,7 +719,8 @@
     panel = vmem((2, half, regions * LANES), bf16)
     sems = pltpu.SemaphoreType.DMA
     scratch = (
-        [vmem((8, cells), f32)]
+        [vmem(t.shape, f32) for t in consts]
+        + [vmem((8, cells), f32)]
         + [vmem((regions, rows, length), f32)] * 2
         + [vmem((device_count, 8, cells), f32)]
         + [basis] * 6
@@ -737,6 +757,7 @@
             sems((3,)),
             sems((2,)),
             sems((2,)),
+            sems((len(consts),)),
         ]
     )
     whole = pl.BlockSpec(memory_space=vmem)
@@ -750,22 +771,22 @@
             jax.ShapeDtypeStruct((2, cells), f32),
             jax.ShapeDtypeStruct((8, LANES), f32),
         ),
-        in_specs=[whole] * (6 + len(consts)),
+        in_specs=[whole] * 6 + [anywhere] * len(consts),
         out_specs=(anywhere, anywhere, whole, whole),
         scratch_shapes=scratch,
         compiler_params=pltpu.CompilerParams(
             collective_id=0, has_side_effects=True, vmem_limit_bytes=67043328
         ),
     )(cell_row, cell_col, cell_width, cell_height, cell_region, cell_offset, *consts)
-    block = pl.BlockSpec((1, rows, length), lambda g: (g, 0, 0))
-    small = pl.BlockSpec((2, cells), lambda g: (0, 0))
-    number = pl.BlockSpec((1, 1), lambda g: (0, 0), memory_space=pltpu.SMEM)
+    block = pl.BlockSpec((1, rows // 2, length), lambda g, r: (g, r, 0))
+    small = pl.BlockSpec((2, cells), lambda g, r: (0, 0))
+    number = pl.BlockSpec((1, 1), lambda g, r: (0, 0), memory_space=pltpu.SMEM)
     single = jax.ShapeDtypeStruct((1, 1), f32)
     field_x, field_y, force, energy, overflow = pl.pallas_call(
         hand_out,
-        grid=(regions,),
+        grid=(regions, 2),
         out_shape=(field, field, jax.ShapeDtypeStruct((2, cells), f32), single, single),
-        in_specs=[block, block, small, pl.BlockSpec((8, LANES), lambda g: (0, 0), memory_space=pltpu.SMEM)],
+        in_specs=[block, block, small, pl.BlockSpec((8, LANES), lambda g, r: (0, 0), memory_space=pltpu.SMEM)],
         out_specs=(block, block, small, number, number),
     )(field_x, field_y, force, scalars)
     return field_x, field_y, force, energy.reshape(()), overflow.reshape(())

time: 92.3 us -> 89.7 us (0.972)
  the two profiles are of different devices: /device:TPU:13 before, /device:TPU:23 now
where the time goes in v2:
time: 89.7 us; the launch traced here: 89.4 us
  Pallas kernels  88.7 us (99%)
    pallas_call x1, Pallas kernels, fused_body(): pl.pallas_call(functools.partial(fused_kernel, slab_count, length, cells,...  82.1 us
    pallas_call x1, Pallas kernels, fused_body(): pl.pallas_call(hand_out, grid=(regions, 2), out_shape=(field, field, jax....  6.62 us

profile of v2, /device:TPU:23, one launch (start us, length us, event | category | flops | bytes accessed | tf_op | source)
XLA Modules:
  0.0 89.4 jit_solution(13778436871411901086)
XLA Ops:
  0.6 82.1 %shard_map.173 = (f32[4,64,2048]{2,1,0:T(8,128)}, f32[4,64,2048]{2,1,0:T(8,128)}, f32[2,512]{1,0:T(2,128)}, f32[8,128]{1,0:T(8,128)}) custom-call(s32[512]{0:T(512)} %cell_row.1, s32[512]{0:T(512)} %cell_col.1, s32[512]{0:T(512)} %cell_width.1, s32[512]{0:T(512)} %cell_height.1, s32[512]{0:T(512)} %cell_region.1, f32[2,512]{1,0:T(2,128)} %cell_offset.1, ...), custom_call_target="tpu_custom_call" | custom-call | tf_op jit(solution)/shard_map/pallas_call | solution.py:766
  82.8 6.6 %shard_map.174 = (f32[4,64,2048]{2,1,0:T(8,128)}, f32[4,64,2048]{2,1,0:T(8,128)}, f32[2,512]{1,0:T(2,128)}, f32[1,1]{1,0:T(1,128)}, f32[1,1]{1,0:T(1,128)}) custom-call(f32[4,64,2048]{2,1,0:T(8,128)} %get-tuple-element.14.in_x, f32[4,64,2048]{2,1,0:T(8,128)} %get-tuple-element.15.in_y, f32[2,512]{1,0:T(2,128)} %get-tuple-element.16.in_force, ...), custom_call_target="tpu_custom_call" | custom-call | tf_op jit(solution)/shard_map/pallas_call | solution.py:785

commit v3 on v2

--- a/solution.py
+++ b/solution.py
@@ -697,12 +697,21 @@
         copy.wait()
 
 
-def hand_out(in_x, in_y, in_force, in_scalars, out_x, out_y, force, energy, overflow):
-    out_x[...] = in_x[...]
-    out_y[...] = in_y[...]
+def hand_out(in_x, in_y, in_force, in_scalars, out_x, out_y, force, energy, overflow, held, in_sem, out_sem):
+    moves = []
+    for index, (source, target) in enumerate(((in_x, out_x), (in_y, out_y))):
+        for g in range(source.shape[0]):
+            inward = pltpu.make_async_copy(source.at[g], held.at[index, g], in_sem.at[index, g])
+            inward.start()
+            moves.append((inward, pltpu.make_async_copy(held.at[index, g], target.at[g], out_sem.at[index, g])))
+    for inward, outward in moves:
+        inward.wait()
+        outward.start()
     force[...] = in_force[...]
     energy[0, 0] = in_scalars[0, 2]
     overflow[0, 0] = in_scalars[0, 3]
+    for _, outward in moves:
+        outward.wait()
 
 
 def fused_body(cell_row, cell_col, cell_width, cell_height, cell_region, cell_offset):
@@ -778,16 +787,14 @@
             collective_id=0, has_side_effects=True, vmem_limit_bytes=67043328
         ),
     )(cell_row, cell_col, cell_width, cell_height, cell_region, cell_offset, *consts)
-    block = pl.BlockSpec((1, rows // 2, length), lambda g, r: (g, r, 0))
-    small = pl.BlockSpec((2, cells), lambda g, r: (0, 0))
-    number = pl.BlockSpec((1, 1), lambda g, r: (0, 0), memory_space=pltpu.SMEM)
+    number = pl.BlockSpec(memory_space=pltpu.SMEM)
     single = jax.ShapeDtypeStruct((1, 1), f32)
     field_x, field_y, force, energy, overflow = pl.pallas_call(
         hand_out,
-        grid=(regions, 2),
         out_shape=(field, field, jax.ShapeDtypeStruct((2, cells), f32), single, single),
-        in_specs=[block, block, small, pl.BlockSpec((8, LANES), lambda g, r: (0, 0), memory_space=pltpu.SMEM)],
-        out_specs=(block, block, small, number, number),
+        in_specs=[anywhere, anywhere, whole, number],
+        out_specs=(anywhere, anywhere, whole, number, number),
+        scratch_shapes=[vmem((2, regions, rows, length), f32), sems((2, regions)), sems((2, regions))],
     )(field_x, field_y, force, scalars)
     return field_x, field_y, force, energy.reshape(()), overflow.reshape(())
 

time: 89.7 us -> 88.1 us (0.982)
  Pallas kernels: 88.7 us -> 87.2 us
    pallas_call x1, Pallas kernels: 6.62 us -> 5.04 us  [fused_body(): pl.pallas_call(hand_out, out_shape=(field, field, jax.ShapeDtypeStruct((2...]
where the time goes in v3:
time: 88.1 us; the launch traced here: 87.8 us
  Pallas kernels  87.2 us (99%)
    pallas_call x1, Pallas kernels, fused_body(): pl.pallas_call(functools.partial(fused_kernel, slab_count, length, cells,...  82.1 us
    pallas_call x1, Pallas kernels, fused_body(): pl.pallas_call(hand_out, out_shape=(field, field, jax.ShapeDtypeStruct((2...  5.04 us

profile of v3, /device:TPU:23, one launch (start us, length us, event | category | flops | bytes accessed | tf_op | source)
XLA Modules:
  0.0 87.8 jit_solution(4457627224065126204)
XLA Ops:
  0.6 82.1 %shard_map.173 = (f32[4,64,2048]{2,1,0:T(8,128)}, f32[4,64,2048]{2,1,0:T(8,128)}, f32[2,512]{1,0:T(2,128)}, f32[8,128]{1,0:T(8,128)}) custom-call(s32[512]{0:T(512)} %cell_row.1, s32[512]{0:T(512)} %cell_col.1, s32[512]{0:T(512)} %cell_width.1, s32[512]{0:T(512)} %cell_height.1, s32[512]{0:T(512)} %cell_region.1, f32[2,512]{1,0:T(2,128)} %cell_offset.1, ...), custom_call_target="tpu_custom_call" | custom-call | tf_op jit(solution)/shard_map/pallas_call | solution.py:775
  82.8 5.0 %shard_map.174 = (f32[4,64,2048]{2,1,0:T(8,128)}, f32[4,64,2048]{2,1,0:T(8,128)}, f32[2,512]{1,0:T(2,128)}, f32[1,1]{1,0:T(1,128)}, f32[1,1]{1,0:T(1,128)}) custom-call(f32[4,64,2048]{2,1,0:T(8,128)} %get-tuple-element.14.in_x, f32[4,64,2048]{2,1,0:T(8,128)} %get-tuple-element.15.in_y, f32[2,512]{1,0:T(2,128)} %get-tuple-element.16.in_force, ...), custom_call_target="tpu_custom_call" | custom-call | tf_op jit(solution)/shard_map/pallas_call | solution.py:792

commit v4 on v3

--- a/solution.py
+++ b/solution.py
@@ -190,6 +190,10 @@
 FINE = 48
 LANES = 128
 CODE_TOP = 32000.0
+NARROW = jnp.float8_e5m2
+LIFT = 256.0
+PANEL_SCALE = 64.0
+HOME_SCALE = 16.0
 
 
 def trig(phase, length):
@@ -218,6 +222,14 @@
     return high, (value - high.astype(jnp.float32)).astype(jnp.bfloat16)
 
 
+def put(high, narrow, at, value, scale=1.0):
+    head = value.astype(jnp.bfloat16)
+    high[at] = head
+    rest = value - head.astype(jnp.float32)
+    narrow[(0,) + at] = (value * scale if scale != 1.0 else value).astype(NARROW)
+    narrow[(1,) + at] = (rest * (LIFT * scale)).astype(NARROW)
+
+
 def dot(left, right, contract=((1,), (0,))):
     return lax.dot_general(left, right, (contract, ((), ())), preferred_element_type=jnp.float32)
 
@@ -242,7 +254,7 @@
     out_x, out_y, force, scalars,
     ccos, csin, fcos, fsin, gcos, gsin, hcos, hsin, table, field_x, field_y, cells_all, xch, xcl, ych, ycl, ysh, ysl, draw, foh, fol, hxh, hxl, hyh, hyl,
     send_buf, send_scale, recv_buf, recv_scale, rounded, xf, xg, carry, yown, ybelow,
-    energy_acc, excess_acc, area_acc, scal_out, scal_in, part_own, part_below, part_sib, part_up,
+    low_columns, energy_acc, excess_acc, area_acc, scal_out, scal_in, part_own, part_below, part_sib, part_up,
     cell_send, cell_recv, data_send, data_recv, scale_send, scale_recv,
     scal_send, scal_recv, part_send, part_recv, out_sem, trig_sem,
 ):
@@ -328,8 +340,8 @@
                 cosine, sine = rotate(
                     ccos[row, lanes], csin[row, lanes], fcos[:INNER, lanes], fsin[:INNER, lanes]
                 )
-                ych[parity, at, out], ycl[parity, at, out] = split(cosine)
-                ysh[parity, at, out], ysl[parity, at, out] = split(sine)
+                put(ych, ycl, (parity, at, out), cosine)
+                put(ysh, ysl, (parity, at, out), sine)
         return 0
 
     def build_x(step, high, low, pick):
@@ -339,7 +351,7 @@
             for part in range(half // 256):
                 lanes = pl.ds(part * 256, 256)
                 value = rotate(gcos[row, lanes], gsin[row, lanes], hcos[parity, :, lanes], hsin[parity, :, lanes])
-                high[parity, at, lanes], low[parity, at, lanes] = split(value[pick])
+                put(high, low, (parity, at, lanes), value[pick])
         return 0
 
     lax.fori_loop(0, half // INNER, lambda s, c: build_x(s, xch, xcl, 0), 0)
@@ -424,8 +436,9 @@
     def fold(step, _):
         at = pl.ds(pl.multiple_of(step * 64, 64), 64)
         lower, upper = draw[0, at, :], draw[1, at, :]
-        foh[0, at, :], fol[0, at, :] = split(lower + upper)
-        foh[1, at, :], fol[1, at, :] = split(lower - upper)
+        every = slice(None)
+        put(foh, fol, (0, at, every), lower + upper)
+        put(foh, fol, (1, at, every), lower - upper)
         return 0
 
     lax.fori_loop(0, half // 64, fold, 0)
@@ -440,8 +453,8 @@
         parity = step // (half // chunk)
         first = (step % (half // chunk)) * chunk
         at = pl.ds(pl.multiple_of(first, chunk), chunk)
-        high, low = xch[parity, at, :], xcl[parity, at, :]
-        spectrum = dot(high, foh[parity]) + (dot(high, fol[parity]) + dot(low, foh[parity]))
+        cross = dot(xcl[0, parity, at, :], fol[1, parity]) + dot(xcl[1, parity, at, :], fol[0, parity])
+        spectrum = dot(xch[parity, at, :], foh[parity]) + cross * (1.0 / LIFT)
         ky = (2 * (first + lax.broadcasted_iota(jnp.int32, (chunk, LANES), 0)) + parity).astype(f32)
         squared = kx * kx + ky * ky
         at_anchor = squared == 0.0
@@ -455,8 +468,8 @@
         for g in range(regions):
             lanes = pl.ds(g * LANES, LANES)
             part = spectrum[:, g * LANES : (g + 1) * LANES]
-            hxh[parity, at, lanes], hxl[parity, at, lanes] = split(part * weight_x)
-            hyh[parity, at, lanes], hyl[parity, at, lanes] = split(part * weight_y)
+            put(hxh, hxl, (parity, at, lanes), part * weight_x, PANEL_SCALE)
+            put(hyh, hyl, (parity, at, lanes), part * weight_y, PANEL_SCALE)
             energy += fold_rows(part * part * weight)
         energy_acc[...] = energy
         return 0
@@ -482,11 +495,13 @@
     def inverse(step, _, index, th, tl, vh, vl):
         tile = (spot // 4 + step + 1) % tiles
         at = pl.ds(pl.multiple_of(tile * (4 * rows), 4 * rows), 4 * rows)
-        value = None
+        value = cross = None
         for parity in range(2):
-            high, low = th[parity, at, :], tl[parity, at, :]
-            term = dot(high, vh[parity]) + (dot(high, vl[parity]) + dot(low, vh[parity]))
+            term = dot(th[parity, at, :], vh[parity])
+            more = dot(tl[0, parity, at, :], vl[1, parity]) + dot(tl[1, parity, at, :], vl[0, parity])
             value = term if value is None else value + term
+            cross = more if cross is None else cross + more
+        value = value + cross * (1.0 / (LIFT * PANEL_SCALE))
         for part in range(4):
             block = value[part * rows : (part + 1) * rows]
             top = jnp.maximum(jnp.max(jnp.abs(block), axis=0, keepdims=True), 1e-30)
@@ -525,7 +540,7 @@
         at = pl.ds(pl.multiple_of(step * 64, 64), 64)
         for part in range(2):
             spots = row_iota(64, both) + (step * 64 + part * half).astype(f32)
-            for ref, (_, col, wide, _, _, off_x, _) in ((ych, own), (ycl, under)):
+            for ref, (_, col, wide, _, _, off_x, _) in ((ych, own), (low_columns, under)):
                 ref[part, at, :] = overlap(spots - col, off_x, wide).astype(bf16)
         return 0
 
@@ -537,7 +552,7 @@
         part = step // (half // 256)
         at = pl.ds(pl.multiple_of((step % (half // 256)) * 256, 256), 256)
         density = dot(yown[...], ych[part, at, :], ((1,), (1,)))
-        extra = dot(ybelow[...], ycl[part, at, :], ((1,), (1,)))
+        extra = dot(ybelow[...], low_columns[part, at, :], ((1,), (1,)))
         excess, area = excess_acc[...], area_acc[...]
         for g in range(regions):
             block = density[g * rows : (g + 1) * rows]
@@ -583,7 +598,7 @@
         value = recv_buf[index, source].astype(jnp.int32).astype(f32) * recv_scale[index, source, :1, :]
         for g in range(regions):
             at = pl.ds(pl.multiple_of(across * (regions * rows) + g * rows, rows), rows)
-            foh[index, at, lanes], fol[index, at, lanes] = split(value[:, g * LANES : (g + 1) * LANES])
+            put(foh, fol, (index, at, lanes), value[:, g * LANES : (g + 1) * LANES], HOME_SCALE)
         return 0
 
     high_rows = regions * rows
@@ -594,15 +609,16 @@
         at = pl.ds(pl.multiple_of(step * wide, wide), wide)
         sums = []
         for parity in range(2):
-            total = None
+            total = cross = None
             for block in range(2):
                 pick = pl.ds((parity * 2 + block) * high_rows, high_rows)
-                high, low = foh[index, pick, :], fol[index, pick, :]
                 depth = pl.ds(block * 512, 512)
-                left, right = th[parity, depth, at], tl[parity, depth, at]
-                term = dot(high, left) + (dot(high, right) + dot(low, left))
+                term = dot(foh[index, pick, :], th[parity, depth, at])
+                more = dot(fol[0, index, pick, :], tl[1, parity, depth, at])
+                more += dot(fol[1, index, pick, :], tl[0, parity, depth, at])
                 total = term if total is None else total + term
-            sums.append(total)
+                cross = more if cross is None else cross + more
+            sums.append(total + cross * (1.0 / (LIFT * HOME_SCALE)))
         even, odd = sums
         straight = even + odd
         back = even - odd if index else odd - even
@@ -627,7 +643,7 @@
         leaving[-1].start()
         low_rows = jnp.concatenate([out[g, :8, :] for g in range(regions)], 0).astype(bf16)
         total = dot(rounded[:, :half], ych[0]) + dot(rounded[:, half:], ych[1])
-        extra = dot(low_rows[:, :half], ycl[0]) + dot(low_rows[:, half:], ycl[1])
+        extra = dot(low_rows[:, :half], low_columns[0]) + dot(low_rows[:, half:], low_columns[1])
         total = jnp.sum(total * yown[...].astype(f32), axis=0, keepdims=True)
         extra = jnp.sum(extra * ybelow[...].astype(f32), axis=0, keepdims=True)
         for part in range(2):
@@ -726,15 +742,17 @@
     vmem = pltpu.VMEM
     basis = vmem((2, half, half), bf16)
     panel = vmem((2, half, regions * LANES), bf16)
+    basis_cross = vmem((2, 2, half, half), NARROW)
+    panel_cross = vmem((2, 2, half, regions * LANES), NARROW)
     sems = pltpu.SemaphoreType.DMA
     scratch = (
         [vmem(t.shape, f32) for t in consts]
         + [vmem((8, cells), f32)]
         + [vmem((regions, rows, length), f32)] * 2
         + [vmem((device_count, 8, cells), f32)]
-        + [basis] * 6
+        + [basis, basis_cross] * 3
         + [vmem((2, half, regions * LANES), f32)]
-        + [panel] * 6
+        + [panel, panel_cross] * 3
         + [
             vmem((2, group, rows, regions * LANES), jnp.int16),
             vmem((2, group, 2, regions * LANES), f32),
@@ -746,6 +764,7 @@
             vmem((slab_count, 8 * regions, LANES), f32),
             vmem((regions * rows, 2 * cells), bf16),
             vmem((8 * regions, 2 * cells), bf16),
+            basis,
             vmem((8, LANES), f32),
             vmem((8, 256), f32),
             vmem((8, 256), f32),

time: 88.1 us -> 85.7 us (0.973)
  the two profiles are of different devices: /device:TPU:23 before, /device:TPU:13 now
where the time goes in v4:
time: 85.7 us; the launch traced here: 85.3 us
  Pallas kernels  84.6 us (99%)
    pallas_call x1, Pallas kernels, fused_body(): pl.pallas_call(functools.partial(fused_kernel, slab_count, length, cells,...  79.6 us
    pallas_call x1, Pallas kernels, fused_body(): pl.pallas_call(hand_out, out_shape=(field, field, jax.ShapeDtypeStruct((2...  5.04 us

profile of v4, /device:TPU:13, one launch (start us, length us, event | category | flops | bytes accessed | tf_op | source)
XLA Modules:
  0.0 85.3 jit_solution(13681243964428134135)
XLA Ops:
  0.6 79.6 %shard_map.173 = (f32[4,64,2048]{2,1,0:T(8,128)}, f32[4,64,2048]{2,1,0:T(8,128)}, f32[2,512]{1,0:T(2,128)}, f32[8,128]{1,0:T(8,128)}) custom-call(s32[512]{0:T(512)} %cell_row.1, s32[512]{0:T(512)} %cell_col.1, s32[512]{0:T(512)} %cell_width.1, s32[512]{0:T(512)} %cell_height.1, s32[512]{0:T(512)} %cell_region.1, f32[2,512]{1,0:T(2,128)} %cell_offset.1, ...), custom_call_target="tpu_custom_call" | custom-call | tf_op jit(solution)/shard_map/pallas_call | solution.py:794
  80.3 5.0 %shard_map.174 = (f32[4,64,2048]{2,1,0:T(8,128)}, f32[4,64,2048]{2,1,0:T(8,128)}, f32[2,512]{1,0:T(2,128)}, f32[1,1]{1,0:T(1,128)}, f32[1,1]{1,0:T(1,128)}) custom-call(f32[4,64,2048]{2,1,0:T(8,128)} %get-tuple-element.14.in_x, f32[4,64,2048]{2,1,0:T(8,128)} %get-tuple-element.15.in_y, f32[2,512]{1,0:T(2,128)} %get-tuple-element.16.in_force, ...), custom_call_target="tpu_custom_call" | custom-call | tf_op jit(solution)/shard_map/pallas_call | solution.py:811
